TPU v7x, 32 devices: a whole 2x2x4 slice. The times are simulated.
32 devices in a mesh: blk: 4 (over x, core), tp: 8 (over z, y).
Axes of the slice: x: 2, y: 2, z: 4, core: 2. Of those that a mesh axis runs over, the one named last changes fastest.
Arguments:
- residual_in: bfloat16 [2048, 5120], P('blk'), may hold values from -6 to 6
- norm_gain: bfloat16 [5120], replicated, may hold values from 0.099609375 to 1.8984375
- w_query: bfloat16 [5120, 4096], P(('blk', 'tp')), may hold values from -0.5 to 0.5
- w_key_value: bfloat16 [5120, 2048], P(('blk', 'tp')), may hold values from -0.5 to 0.5
- query_bias: bfloat16 [4096], replicated, may hold values from -3 to 3
- key_value_bias: bfloat16 [2048], replicated, may hold values from -3 to 3
- w_output: bfloat16 [4096, 5120], P(None, ('blk', 'tp')), may hold values from -0.09375 to 0.09375
- device_map: int32 [32], replicated, may hold values from 0 to 31, each once
- positions: int32 [2048], P('blk'), may hold values from 0 to 4094, as said below
- segments: int32 [2048], P('blk'), may hold values from 0 to 1, as said below
Outputs:
- output: bfloat16 [2048, 5120], P('blk', 'tp')
Inputs may be any that keep to these rules, and one draw needn't show every extreme that they name: `segments`: ids never fall; both ids 0 and 1 occur; the shorter prompt holds a quarter of 512 up to 511 tokens. `positions`: a token's index within its prompt plus an offset shared by the whole prompt; the longer prompt's last token stands at 4094. `device_map`: each of 0 to 31 once.
All inputs are finite; a program needn't handle non-finite values.
Results may differ from a plain program's by a relative error of at most 0.012.
Values may be sent and summed in bfloat16 or wider, within the bound.
No kernel may reach another device: no remote copies, remote signals or barrier semaphores. Data moves between devices by JAX's collectives and lax.ppermute only.
A program may use at most 128 MiB of HBM per device.

v0:
```python
import jax
import jax.numpy as jnp
from jax import lax
from jax.sharding import PartitionSpec as P

D = 5120
KVH = 8
HD = 128
NORM_FLOOR = 0.0625
ROPE_BASE = 1000000.0
NEGATIVE_FILL = -1e30


def for_sending(x):
    return jax.tree.map(lambda a: a.astype(jnp.bfloat16) if a.dtype == jnp.float32 else a, x)


def from_partner(block, axis, bit):
    count = lax.axis_size(axis)
    route = []
    for low in range(count):
        high = low | 1 << bit
        if high != low and high < count:
            route += [(low, high), (high, low)]
    return lax.ppermute(block, axis, route)


def rope_tables(positions, head_width):
    half_width = head_width // 2
    frequency = ROPE_BASE ** (-(jnp.arange(half_width, dtype=jnp.float32) * 2.0) / head_width)
    angles = positions.astype(jnp.float32)[:, None] * frequency[None, :]
    angles = jnp.concatenate([angles, angles], axis=1)
    return (jnp.cos(angles), jnp.sin(angles))


def rotate(values, cosine_table, sine_table):
    half_width = values.shape[-1] // 2
    turned = jnp.concatenate([-values[..., half_width:], values[..., :half_width]], axis=-1)
    return values * cosine_table[:, None, :] + turned * sine_table[:, None, :]


def join_pair(mine_cols, partner, is_lower):
    return jnp.where(
        is_lower,
        jnp.concatenate([mine_cols, partner], axis=1),
        jnp.concatenate([partner, mine_cols], axis=1),
    )


def per_device(
    residual_in,
    norm_gain,
    w_query,
    w_key_value,
    query_bias,
    key_value_bias,
    w_output,
    device_map,
    positions,
    segments,
):
    tp_count = lax.axis_size("tp")
    tp_index = lax.axis_index("tp")
    blk_index = lax.axis_index("blk")
    local_tokens = residual_in.shape[0]
    shard_rows = w_query.shape[0]
    kv_group = tp_count // KVH
    floats = residual_in.astype(jnp.float32)
    square = jnp.maximum(jnp.mean(floats * floats, axis=1, keepdims=True), NORM_FLOOR)
    normed = (floats * lax.rsqrt(square) * norm_gain.astype(jnp.float32)).astype(jnp.bfloat16)
    ordered = jnp.take(
        normed.reshape(local_tokens, device_map.shape[0], shard_rows), device_map, axis=1
    ).reshape(local_tokens, D)
    moved_query, moved_pairs = (
        lax.all_to_all(w_query, "tp", split_axis=1, concat_axis=0, tiled=True),
        lax.all_to_all(w_key_value, "tp", split_axis=1, concat_axis=0, tiled=True),
    )
    for bit_level in range(kv_group.bit_length() - 1):
        partner = from_partner(for_sending(moved_pairs), "tp", bit_level).astype(moved_pairs.dtype)
        moved_pairs = join_pair(moved_pairs, partner, tp_index >> bit_level & 1 == 0)
    queries = jnp.dot(
        ordered,
        lax.all_gather(moved_query, "blk", axis=0, tiled=True),
        preferred_element_type=jnp.float32,
    )
    key_value = jnp.dot(
        ordered,
        lax.all_gather(moved_pairs, "blk", axis=0, tiled=True),
        preferred_element_type=jnp.float32,
    )
    query_width = queries.shape[1]
    heads_here = query_width // HD
    kv_head = tp_index // kv_group
    queries = queries + lax.dynamic_slice_in_dim(
        query_bias, tp_index * query_width, query_width
    ).astype(jnp.float32)
    key_value = key_value + lax.dynamic_slice_in_dim(
        key_value_bias, kv_head * 2 * HD, 2 * HD
    ).astype(jnp.float32)
    cosine_table, sine_table = rope_tables(positions, HD)
    query_rot = rotate(
        queries.reshape(local_tokens, heads_here, HD), cosine_table, sine_table
    ).astype(jnp.bfloat16)
    key_rot = rotate(key_value[:, None, :HD], cosine_table, sine_table)[:, 0, :].astype(
        jnp.bfloat16
    )
    values = key_value[:, HD:].astype(jnp.bfloat16)
    attend_scale = HD ** (-0.5)
    row_index = blk_index * local_tokens + jnp.arange(local_tokens, dtype=jnp.int32)
    initial = (
        jnp.full((heads_here, local_tokens), NEGATIVE_FILL, jnp.float32),
        jnp.zeros((heads_here, local_tokens), jnp.float32),
        jnp.zeros((heads_here, local_tokens, HD), jnp.float32),
    )
    key_piece = lax.all_gather(key_rot, "blk", axis=0, tiled=True)
    value_piece = lax.all_gather(values, "blk", axis=0, tiled=True)
    segment_piece = lax.all_gather(segments, "blk", axis=0, tiled=True)
    piece_rows = key_piece.shape[0]
    key_block_rows = 512

    def one_block(block_number, state_now):
        run_peak, run_mass, context = state_now
        block_start = block_number * key_block_rows
        key_block = lax.dynamic_slice_in_dim(key_piece, block_start, key_block_rows, 0)
        value_block = lax.dynamic_slice_in_dim(value_piece, block_start, key_block_rows, 0)
        segment_block = lax.dynamic_slice_in_dim(segment_piece, block_start, key_block_rows, 0)
        scores = (
            jnp.einsum("qhd,kd->hqk", query_rot, key_block, preferred_element_type=jnp.float32)
            * attend_scale
        )
        key_index = block_start + jnp.arange(key_block_rows, dtype=jnp.int32)
        visible = (key_index[None, :] <= row_index[:, None]) & (
            segment_block[None, :] == segments[:, None]
        )
        masked = jnp.where(visible[None], scores, NEGATIVE_FILL)
        new_peak = jnp.maximum(run_peak, jnp.max(masked, axis=2))
        factor = jnp.exp(run_peak - new_peak)
        raw_weights = jnp.where(visible[None], jnp.exp(masked - new_peak[:, :, None]), 0.0)
        run_mass = run_mass * factor + jnp.sum(raw_weights, axis=2)
        context = context * factor[:, :, None] + jnp.einsum(
            "hqk,kd->hqd",
            raw_weights.astype(jnp.bfloat16),
            value_block,
            preferred_element_type=jnp.float32,
        )
        return (new_peak, run_mass, context)

    run_peak, run_mass, context = lax.fori_loop(0, piece_rows // key_block_rows, one_block, initial)
    context_flat = (
        (context / run_mass[:, :, None])
        .transpose(1, 0, 2)
        .reshape(local_tokens, query_width)
        .astype(jnp.bfloat16)
    )
    width_out = D // tp_count
    moved_out = lax.all_to_all(w_output, "tp", split_axis=0, concat_axis=1, tiled=True)
    row_terms = jnp.dot(
        context_flat,
        lax.all_gather(moved_out, "blk", axis=1, tiled=True),
        preferred_element_type=jnp.float32,
    )
    summed = lax.psum_scatter(
        row_terms.astype(jnp.bfloat16), "tp", scatter_dimension=1, tiled=True
    ).astype(jnp.float32)
    residual_part = lax.dynamic_slice_in_dim(residual_in, tp_index * width_out, width_out, 1)
    return (residual_part.astype(jnp.float32) + summed).astype(jnp.bfloat16)


def solution(mesh):
    in_specs = (
        P("blk", None),
        P(),
        P(("blk", "tp"), None),
        P(("blk", "tp"), None),
        P(),
        P(),
        P(None, ("blk", "tp")),
        P(),
        P("blk"),
        P("blk"),
    )
    out_specs = P("blk", "tp")
    return jax.shard_map(
        per_device, mesh=mesh, in_specs=in_specs, out_specs=out_specs, check_vma=False
    )
```

profile of v0, /device:TPU:0, one launch (start us, length us, event | category | flops | bytes accessed | tf_op | source)
XLA Modules:
  0.0 321.4 jit_solution(14802717648949575570)
XLA Ops:
  6.5 1.1 copy.68
  7.7 25.0 %all_to_all.57 = bf16[160,8,256]{2,0,1:T(8,128)(2,1)} all-to-all(bf16[160,8,256]{2,0,1:T(8,128)(2,1)S(1)} %bitcast.88), channel_id=1, replica_groups=mesh['blk'=4,'tp'=8] {'tp'}, dimensions={1} | all-to-all | bytes 1310720 | tf_op jit(solution)/shard_map/all_to_all | solution.py:76
  32.8 1.4 copy.67
  34.2 34.4 %all_to_all.58 = bf16[160,8,512]{2,0,1:T(8,128)(2,1)} all-to-all(bf16[160,8,512]{2,0,1:T(8,128)(2,1)S(1)} %bitcast.86), channel_id=1, replica_groups=mesh['blk'=4,'tp'=8] {'tp'}, dimensions={1} | all-to-all | bytes 2621440 | tf_op jit(solution)/shard_map/all_to_all | solution.py:75
  68.6 1.3 copy.66
  69.9 3.6 %all-to-all-start.2 = ((bf16[8,512,160]{1,2,0:T(8,128)(2,1)}), bf16[8,512,160]{1,2,0:T(8,128)(2,1)S(1)}, u32[]{:S(2)}, u32[]{:S(2)}) async-start(bf16[8,512,160]{1,2,0:T(8,128)(2,1)} %bitcast.67), calls=%async_computation.2 | async-start | bytes 2621440 | tf_op jit(solution)/shard_map/all_to_all | solution.py:156
  73.5 8.1 %copy.43 = bf16[512,5120]{0,1:T(8,128)(2,1)} copy(bf16[512,5120]{1,0:T(8,128)(2,1)} %param.12) | data formatting | bytes 10485760 | tf_op args[0]
  81.7 3.8 %fusion.22 = f32[512]{0:T(512)S(1)} fusion(bf16[512,5120]{0,1:T(8,128)(2,1)} %copy.43), kind=kLoop, calls=%fused_computation.30 | loop fusion | flops 7863808 | bytes 5244928 | tf_op jit(solution)/shard_map/reduce_sum | solution.py:69
  85.8 3.9 %fusion.24 = bf16[512,5120]{0,1:T(8,128)(2,1)} fusion(bf16[512,5120]{0,1:T(8,128)(2,1)S(1)} %copy-done.1, f32[5120]{0:T(1024)S(1)} %convert_element_type.55, f32[512]{0:T(512)S(1)} %maximum_rsqrt_fusion), kind=kLoop, calls=%fused_computation.32 | loop fusion | flops 10485760 | bytes 10508288 | tf_op jit(solution)/shard_map/convert_element_type | solution.py:70
  90.0 5.6 %gather_fusion = bf16[32,512,160]{1,2,0:T(8,128)(2,1)} fusion(bf16[512,32,160]{0,2,1:T(8,128)(2,1)} %bitcast.82, s32[1024]{0:T(1024)S(1)} %pad_clamp_fusion), kind=kCustom, calls=%fused_computation | custom fusion | bytes 10485888 | tf_op jit(solution)/shard_map/jit(_take)/gather | solution.py:71
  95.6 5.3 %all-gather = s32[4,1,512]{2,1,0:T(1,128)S(1)} all-gather(s32[1,1,512]{2,1,0:T(1,128)S(1)} %bitcast.95), channel_id=1, replica_groups=mesh['blk'=4,'tp'=8] {'blk'}, dimensions={0}, use_global_device_ids=true | all-gather | bytes 10240 | tf_op jit(solution)/shard_map/all_gather | solution.py:117
  101.0 0.8 dynamic-slice_convert_fusion.1
  101.7 0.8 dynamic-slice_convert_fusion
  102.6 7.1 %bitcast_select_fusion.1 = bf16[512,5120]{0,1:T(8,128)(2,1)} fusion(bf16[32,512,160]{1,2,0:T(8,128)(2,1)} %gather_fusion, pred[5120]{0:T(1024)(128)(4,1)S(1)} %broadcast_in_dim.101), kind=kLoop, calls=%fused_computation.34 | loop fusion | flops 2621440 | bytes 10490880 | tf_op jit(solution)/shard_map/jit(_take)/select_n | solution.py:71
  109.7 1.1 copy-done.2
  110.8 4.9 %convolution_add_fusion.1 = f32[512,256]{0,1:T(8,128)S(1)} fusion(bf16[512,5120]{0,1:T(8,128)(2,1)} %bitcast_select_fusion.1, bf16[5120,256]{1,0:T(8,128)(2,1)} %all-gather.5.cloned.1.call-done, f32[256]{0:T(256)S(1)} %dynamic-slice_convert_fusion.1), kind=kOutput, calls=%fused_computation.39 | convolution fusion | flops 1342308352 | bytes 8389632 | tf_op jit(solution)/shard_map/dot_general | solution.py:86
  115.8 1.0 fusion.28
  117.1 8.4 %all_gather.20 = bf16[2048,128]{0,1:T(8,128)(2,1)S(1)} all-gather(bf16[512,128]{0,1:T(8,128)(2,1)S(1)} %get-tuple-element.284), channel_id=1, replica_groups=mesh['blk'=4,'tp'=8] {'blk'}, dimensions={0}, use_global_device_ids=true | all-gather | bytes 655360 | tf_op jit(solution)/shard_map/all_gather | solution.py:115
  125.5 12.1 %all_gather.22 = bf16[2048,128]{0,1:T(8,128)(2,1)} all-gather(bf16[512,128]{0,1:T(8,128)(2,1)S(1)} %slice.41), channel_id=1, replica_groups=mesh['blk'=4,'tp'=8] {'blk'}, dimensions={0}, use_global_device_ids=true | all-gather | bytes 655360 | tf_op jit(solution)/shard_map/all_gather | solution.py:116
  137.6 8.0 %convolution_add_fusion = f32[512,512]{0,1:T(8,128)} fusion(bf16[512,5120]{0,1:T(8,128)(2,1)} %bitcast_select_fusion.1, bf16[5120,512]{1,0:T(8,128)(2,1)} %all-gather.7.cloned.1.call-done, f32[512]{0:T(512)S(1)} %dynamic-slice_convert_fusion), kind=kOutput, calls=%fused_computation.38 | convolution fusion | flops 2684616704 | bytes 11536384 | tf_op jit(solution)/shard_map/dot_general | solution.py:81
  145.6 1.5 copy.47
  147.1 0.3 slice_negate_fusion
  147.5 0.4 fusion.26
  147.9 41.7 %while.18 = (s32[]{:T(128)}, f32[4,512]{1,0:T(4,128)S(1)}, f32[4,512]{1,0:T(4,128)S(1)}, f32[4,512,128]{2,1,0:T(8,128)}, s32[2048]{0:T(1024)S(1)}, /*index=5*/s3...) while((s32[]{:T(128)}, f32[4,512]{1,0:T(4,128)S(1)}, ...), condition=%wide.region_4.5_spmd.clone, body=%wide.region_1.4_spmd.clone.sunk | while | flops 552086528 | bytes 41828644 | solution.py:148
  148.0 0.3 compare_and_fusion.3
  148.3 2.9 fusion.49
  151.2 3.4 %fusion.50 = f32[4,512]{1,0:T(4,128)S(1)} fusion(f32[512,512,4]{1,0,2:T(8,128)} %get-tuple-element.356, f32[4,512]{1,0:T(4,128)S(1)} %select_maximum_fusion.2, pred[512,512]{0,1:T(8,128)(4,1)S(1)} %compare_and_fusion.3), kind=kLoop, calls=%fused_computation.6.clone.1 | loop fusion | flops 5240832 | bytes 4472832 | tf_op jit(solution)/shard_map/while/body/eval_jaxpr/reduce_sum | solution.py:139
  154.7 2.6 fusion.52
  157.4 1.0 copy-done.5
  158.4 0.3 compare_and_fusion.3
  158.7 3.0 fusion.49
  161.7 3.4 %fusion.50 = f32[4,512]{1,0:T(4,128)S(1)} fusion(f32[512,512,4]{1,0,2:T(8,128)} %get-tuple-element.356, f32[4,512]{1,0:T(4,128)S(1)} %select_maximum_fusion.2, pred[512,512]{0,1:T(8,128)(4,1)S(1)} %compare_and_fusion.3), kind=kLoop, calls=%fused_computation.6.clone.1 | loop fusion | flops 5240832 | bytes 4472832 | tf_op jit(solution)/shard_map/while/body/eval_jaxpr/reduce_sum | solution.py:139
  165.1 2.6 fusion.52
  167.8 1.0 copy-done.5
  169.1 2.9 fusion.49
  172.1 3.4 %fusion.50 = f32[4,512]{1,0:T(4,128)S(1)} fusion(f32[512,512,4]{1,0,2:T(8,128)} %get-tuple-element.356, f32[4,512]{1,0:T(4,128)S(1)} %select_maximum_fusion.2, pred[512,512]{0,1:T(8,128)(4,1)S(1)} %compare_and_fusion.3), kind=kLoop, calls=%fused_computation.6.clone.1 | loop fusion | flops 5240832 | bytes 4472832 | tf_op jit(solution)/shard_map/while/body/eval_jaxpr/reduce_sum | solution.py:139
  175.5 2.6 fusion.52
  178.2 1.0 copy-done.5
  179.5 2.9 fusion.49
  182.5 3.4 %fusion.50 = f32[4,512]{1,0:T(4,128)S(1)} fusion(f32[512,512,4]{1,0,2:T(8,128)} %get-tuple-element.356, f32[4,512]{1,0:T(4,128)S(1)} %select_maximum_fusion.2, pred[512,512]{0,1:T(8,128)(4,1)S(1)} %compare_and_fusion.3), kind=kLoop, calls=%fused_computation.6.clone.1 | loop fusion | flops 5240832 | bytes 4472832 | tf_op jit(solution)/shard_map/while/body/eval_jaxpr/reduce_sum | solution.py:139
  185.9 2.6 fusion.52
  188.6 1.0 copy-done.5
  189.6 1.6 copy.53
  191.3 7.3 %convolution_convert_fusion = bf16[512,5120]{1,0:T(8,128)(2,1)} fusion(bf16[512,512]{0,1:T(8,128)(2,1)S(1)} %bitcast.94, bf16[512,5120]{0,1:T(8,128)(2,1)} %all-gather.9.cloned.1.call-done), kind=kOutput, calls=%fused_computation.33 | convolution fusion | flops 2686976000 | bytes 11010048 | tf_op jit(solution)/shard_map/dot_general | solution.py:157
  198.6 7.9 %copy.56 = bf16[512,5120]{0,1:T(8,128)(2,1)} copy(bf16[512,5120]{1,0:T(8,128)(2,1)} %convolution_convert_fusion) | data formatting | bytes 10485760
  206.6 104.8 %reduce-scatter.4.cloned.1.call-done = bf16[640,512]{1,0:T(8,128)(2,1)} async-done(((bf16[5120,512]{1,0:T(8,128)(2,1)}), bf16[640,512]{1,0:T(8,128)(2,1)}) %reduce-scatter.4.cloned.1.call-update) | async-done | bytes 655376
  311.4 1.4 copy.57
  312.8 2.1 add_convert_fusion
  (86 shorter events, 2.3 us)
Async XLA Ops:
  6.5 104.3 %all-gather.5.cloned.1.call-start = ((), (), s32[]{:S(2)}) async-start(), calls=%async_computation.4 | async-start | bytes 3276800 | tf_op jit(solution)/shard_map/all_gather | solution.py:88
  7.7 60.9 %copy-start.3 = (bf16[4096,160]{0,1:T(8,128)(2,1)S(1)}, bf16[4096,160]{0,1:T(8,128)(2,1)}, u32[]{:S(2)}) copy-start(bf16[4096,160]{0,1:T(8,128)(2,1)} %param.18) | copy-start | bytes 3932164
  32.7 104.9 %all-gather.7.cloned.1.call-start = ((), (), s32[]{:S(2)}) async-start(), calls=%async_computation.5 | async-start | bytes 6553600 | tf_op jit(solution)/shard_map/all_gather | solution.py:83
  69.9 39.8 %all-to-all-start.2 = ((bf16[8,512,160]{1,2,0:T(8,128)(2,1)}), bf16[8,512,160]{1,2,0:T(8,128)(2,1)S(1)}, u32[]{:S(2)}, u32[]{:S(2)}) async-start(bf16[8,512,160]{1,2,0:T(8,128)(2,1)} %bitcast.67), calls=%async_computation.2 | async-start | bytes 2621440 | tf_op jit(solution)/shard_map/all_to_all | solution.py:156
  73.5 8.2 %copy-start.7 = (bf16[5120]{0:T(1024)(128)(2,1)S(1)}, bf16[5120]{0:T(1024)(128)(2,1)}, u32[]{:S(2)}) copy-start(bf16[5120]{0:T(1024)(128)(2,1)} %param.13) | copy-start | bytes 30724
  73.5 117.8 %all-gather.9.cloned.1.call-start = ((), (), s32[]{:S(2)}) async-start(), calls=%async_computation.6 | async-start | bytes 6553600 | tf_op jit(solution)/shard_map/all_gather | solution.py:159
  81.6 4.1 %copy-start.1 = (bf16[512,5120]{0,1:T(8,128)(2,1)S(1)}, bf16[512,5120]{0,1:T(8,128)(2,1)}, u32[]{:S(2)}) copy-start(bf16[512,5120]{0,1:T(8,128)(2,1)} %copy.43) | copy-start | bytes 15728644
  85.7 3.9 %copy-start.9 = (s32[32]{0:T(128)S(1)}, s32[32]{0:T(128)}, u32[]{:S(2)}) copy-start(s32[32]{0:T(128)} %param.19) | copy-start | bytes 388
  85.7 4.2 %copy-start.8 = (s32[512]{0:T(512)S(1)}, s32[512]{0:T(512)}, u32[]{:S(2)}) copy-start(s32[512]{0:T(512)} %param.20) | copy-start | bytes 6148
  90.0 5.6 %copy-start.6 = (s32[512]{0:T(512)S(1)}, s32[512]{0:T(512)}, u32[]{:S(2)}) copy-start(s32[512]{0:T(512)} %param.21) | copy-start | bytes 6148
  109.7 1.1 copy-start.2
  110.8 200.6 %reduce-scatter.4.cloned.1.call-start = ((), (), s32[]{:S(2)}) async-start(), calls=%async_computation.7 | async-start | bytes 5898240
  148.3 6.4 %copy-start.4 = (f32[4,512,128]{2,1,0:T(8,128)S(1)}, f32[4,512,128]{2,1,0:T(8,128)}, u32[]{:S(2)}) copy-start(f32[4,512,128]{2,1,0:T(8,128)} %get-tuple-element.376) | copy-start | bytes 3145732 | tf_op jit(solution)/shard_map/while
  151.2 3.5 %copy-start = (f32[512,512,4]{1,0,2:T(8,128)S(1)}, f32[512,512,4]{1,0,2:T(8,128)}, u32[]{:S(2)}) copy-start(f32[512,512,4]{1,0,2:T(8,128)} %get-tuple-element.356) | copy-start | bytes 12582916 | tf_op jit(solution)/shard_map/while
  157.4 1.0 copy-start.5
  158.7 6.4 %copy-start.4 = (f32[4,512,128]{2,1,0:T(8,128)S(1)}, f32[4,512,128]{2,1,0:T(8,128)}, u32[]{:S(2)}) copy-start(f32[4,512,128]{2,1,0:T(8,128)} %get-tuple-element.376) | copy-start | bytes 3145732 | tf_op jit(solution)/shard_map/while
  161.7 3.4 %copy-start = (f32[512,512,4]{1,0,2:T(8,128)S(1)}, f32[512,512,4]{1,0,2:T(8,128)}, u32[]{:S(2)}) copy-start(f32[512,512,4]{1,0,2:T(8,128)} %get-tuple-element.356) | copy-start | bytes 12582916 | tf_op jit(solution)/shard_map/while
  167.8 1.0 copy-start.5
  169.1 6.4 %copy-start.4 = (f32[4,512,128]{2,1,0:T(8,128)S(1)}, f32[4,512,128]{2,1,0:T(8,128)}, u32[]{:S(2)}) copy-start(f32[4,512,128]{2,1,0:T(8,128)} %get-tuple-element.376) | copy-start | bytes 3145732 | tf_op jit(solution)/shard_map/while
  172.1 3.4 %copy-start = (f32[512,512,4]{1,0,2:T(8,128)S(1)}, f32[512,512,4]{1,0,2:T(8,128)}, u32[]{:S(2)}) copy-start(f32[512,512,4]{1,0,2:T(8,128)} %get-tuple-element.356) | copy-start | bytes 12582916 | tf_op jit(solution)/shard_map/while
  178.2 1.0 copy-start.5
  179.5 6.4 %copy-start.4 = (f32[4,512,128]{2,1,0:T(8,128)S(1)}, f32[4,512,128]{2,1,0:T(8,128)}, u32[]{:S(2)}) copy-start(f32[4,512,128]{2,1,0:T(8,128)} %get-tuple-element.376) | copy-start | bytes 3145732 | tf_op jit(solution)/shard_map/while
  182.5 3.4 %copy-start = (f32[512,512,4]{1,0,2:T(8,128)S(1)}, f32[512,512,4]{1,0,2:T(8,128)}, u32[]{:S(2)}) copy-start(f32[512,512,4]{1,0,2:T(8,128)} %get-tuple-element.356) | copy-start | bytes 12582916 | tf_op jit(solution)/shard_map/while
  188.6 1.0 copy-start.5
Sparse Core Ops, SparseCore 0:
  32.8 24.1 all-gather.4
  68.7 39.4 all-gather.6
  110.9 45.1 all-gather.8
  206.7 104.6 reduce-scatter.3
where the time goes:
time: 322 us; the launch traced here: 321 us
  waiting for transfers between devices  105 us (33%)
  blocking collectives  85.3 us (26%)
  matrix products  42.5 us (13%)
  local copies, waits for them, and re-layouts  36 us (11%)
  other arithmetic  35.4 us (11%)
  between operations  13.4 us (4%)
  starting transfers between devices  3.72 us (1%)
    unnamed x5, waiting for transfers between devices  105 us
    all_to_all x1, blocking collectives, per_device(): lax.all_to_all(w_query, 'tp', split_axis=1, concat_axis=0, tiled=True)  34.4 us
    all_to_all x1, blocking collectives, per_device(): lax.all_to_all(w_key_value, 'tp', split_axis=1, concat_axis=0, tiled=True)  25 us
    unnamed x17, local copies, waits for them, and re-layouts  18.7 us
    reduce_sum x4, other arithmetic, one_block(): run_mass = run_mass * factor + jnp.sum(raw_weights, axis=2)  13.6 us
    all_gather x1, blocking collectives, per_device(): value_piece = lax.all_gather(values, 'blk', axis=0, tiled=True)  12.1 us
    dot_general x4, matrix products, one_block(): jnp.einsum('qhd,kd->hqk', query_rot, key_block, preferred_element_type=jn...  11.8 us
    dot_general x4, matrix products, one_block(): jnp.einsum('hqk,kd->hqd', raw_weights.astype(jnp.bfloat16), value_block,...  10.6 us
  transfers between devices with their start and end apart: 5, of which 1 were waited for; matrix products, arithmetic and copies ran while one was open for 28% of the time, Pallas kernels for 0%

commit v1 on v0

--- a/solution.py
+++ b/solution.py
@@ -72,7 +72,10 @@
         normed.reshape(local_tokens, device_map.shape[0], shard_rows), device_map, axis=1
     ).reshape(local_tokens, D)
     moved_query, moved_pairs = (
-        lax.all_to_all(w_query, "tp", split_axis=1, concat_axis=0, tiled=True),
+        jnp.concatenate(
+            lax.all_to_all(jnp.stack(jnp.split(w_query, lax.axis_size("tp"), axis=1)), "tp", 0, 0),
+            axis=0,
+        ),
         lax.all_to_all(w_key_value, "tp", split_axis=1, concat_axis=0, tiled=True),
     )
     for bit_level in range(kv_group.bit_length() - 1):

time: 322 us -> 324 us (level)
    unnamed x17 -> x26, local copies, waits for them, and re-layouts: 18.7 us -> 21.6 us
where the time goes in v1:
time: 324 us; the launch traced here: 323 us
  waiting for transfers between devices  105 us (32%)
  blocking collectives  85.3 us (26%)
  matrix products  42.5 us (13%)
  local copies, waits for them, and re-layouts  37.6 us (12%)
  other arithmetic  35.4 us (11%)
  between operations  13.4 us (4%)
  starting transfers between devices  3.72 us (1%)
    unnamed x5, waiting for transfers between devices  105 us
    all_to_all x1, blocking collectives, per_device(): lax.all_to_all(jnp.stack(jnp.split(w_query, lax.axis_size('tp'), axis=1))...  34.4 us
    all_to_all x1, blocking collectives, per_device(): lax.all_to_all(w_key_value, 'tp', split_axis=1, concat_axis=0, tiled=True)  25 us
    unnamed x26, local copies, waits for them, and re-layouts  21.6 us
    reduce_sum x4, other arithmetic, one_block(): run_mass = run_mass * factor + jnp.sum(raw_weights, axis=2)  13.6 us
    all_gather x1, blocking collectives, per_device(): value_piece = lax.all_gather(values, 'blk', axis=0, tiled=True)  12.1 us
    dot_general x4, matrix products, one_block(): jnp.einsum('qhd,kd->hqk', query_rot, key_block, preferred_element_type=jn...  11.8 us
    dot_general x4, matrix products, one_block(): jnp.einsum('hqk,kd->hqd', raw_weights.astype(jnp.bfloat16), value_block,...  10.6 us
  transfers between devices with their start and end apart: 5, of which 1 were waited for; matrix products, arithmetic and copies ran while one was open for 28% of the time, Pallas kernels for 0%

profile of v1, /device:TPU:0, one launch (start us, length us, event | category | flops | bytes accessed | tf_op | source)
XLA Modules:
  0.0 323.1 jit_solution(3521596972250779837)
XLA Ops:
  6.5 1.2 copy.63
  7.8 25.0 %all_to_all.43 = bf16[160,8,256]{2,0,1:T(8,128)(2,1)} all-to-all(bf16[160,8,256]{2,0,1:T(8,128)(2,1)S(1)} %bitcast.97), channel_id=1, replica_groups=mesh['blk'=4,'tp'=8] {'tp'}, dimensions={1} | all-to-all | bytes 1310720 | tf_op jit(solution)/shard_map/all_to_all | solution.py:79
  32.9 0.9 bitcast_dynamic-update-slice_fusion.7
  33.8 0.9 bitcast_dynamic-update-slice_fusion.6
  34.7 0.9 bitcast_dynamic-update-slice_fusion.5
  35.8 34.4 %all_to_all.44 = bf16[8,160,512]{2,1,0:T(8,128)(2,1)} all-to-all(bf16[8,160,512]{2,1,0:T(8,128)(2,1)S(1)} %bitcast_dynamic-update-slice_fusion), channel_id=1, replica_groups=mesh['blk'=4,'tp'=8] {'tp'}, dimensions={0} | all-to-all | bytes 2621440 | tf_op jit(solution)/shard_map/all_to_all | solution.py:76
  70.2 1.3 copy.62
  71.5 3.6 %all-to-all-start.2 = ((bf16[8,512,160]{1,2,0:T(8,128)(2,1)}), bf16[8,512,160]{1,2,0:T(8,128)(2,1)S(1)}, u32[]{:S(2)}, u32[]{:S(2)}) async-start(bf16[8,512,160]{1,2,0:T(8,128)(2,1)} %bitcast.78), calls=%async_computation.2 | async-start | bytes 2621440 | tf_op jit(solution)/shard_map/all_to_all | solution.py:159
  75.1 8.1 %copy.42 = bf16[512,5120]{0,1:T(8,128)(2,1)} copy(bf16[512,5120]{1,0:T(8,128)(2,1)} %param.12) | data formatting | bytes 10485760 | tf_op args[0]
  83.3 3.8 %fusion.22 = f32[512]{0:T(512)S(1)} fusion(bf16[512,5120]{0,1:T(8,128)(2,1)} %copy.42), kind=kLoop, calls=%fused_computation.30 | loop fusion | flops 7863808 | bytes 5244928 | tf_op jit(solution)/shard_map/reduce_sum | solution.py:69
  87.4 3.9 %fusion.24 = bf16[512,5120]{0,1:T(8,128)(2,1)} fusion(bf16[512,5120]{0,1:T(8,128)(2,1)S(1)} %copy-done.1, f32[5120]{0:T(1024)S(1)} %convert_element_type.55, f32[512]{0:T(512)S(1)} %maximum_rsqrt_fusion), kind=kLoop, calls=%fused_computation.32 | loop fusion | flops 10485760 | bytes 10508288 | tf_op jit(solution)/shard_map/convert_element_type | solution.py:70
  91.6 5.6 %gather_fusion = bf16[32,512,160]{1,2,0:T(8,128)(2,1)} fusion(bf16[512,32,160]{0,2,1:T(8,128)(2,1)} %bitcast.92, s32[1024]{0:T(1024)S(1)} %pad_clamp_fusion), kind=kCustom, calls=%fused_computation | custom fusion | bytes 10485888 | tf_op jit(solution)/shard_map/jit(_take)/gather | solution.py:71
  97.2 5.3 %all-gather = s32[4,1,512]{2,1,0:T(1,128)S(1)} all-gather(s32[1,1,512]{2,1,0:T(1,128)S(1)} %bitcast.103), channel_id=1, replica_groups=mesh['blk'=4,'tp'=8] {'blk'}, dimensions={0}, use_global_device_ids=true | all-gather | bytes 10240 | tf_op jit(solution)/shard_map/all_gather | solution.py:120
  102.6 0.8 dynamic-slice_convert_fusion.1
  103.3 0.8 dynamic-slice_convert_fusion
  104.2 7.1 %bitcast_select_fusion.1 = bf16[512,5120]{0,1:T(8,128)(2,1)} fusion(bf16[32,512,160]{1,2,0:T(8,128)(2,1)} %gather_fusion, pred[5120]{0:T(1024)(128)(4,1)S(1)} %broadcast_in_dim.101), kind=kLoop, calls=%fused_computation.34 | loop fusion | flops 2621440 | bytes 10490880 | tf_op jit(solution)/shard_map/jit(_take)/select_n | solution.py:71
  111.3 1.1 copy-done.2
  112.5 4.9 %convolution_add_fusion.1 = f32[512,256]{0,1:T(8,128)S(1)} fusion(bf16[512,5120]{0,1:T(8,128)(2,1)} %bitcast_select_fusion.1, bf16[5120,256]{1,0:T(8,128)(2,1)} %all-gather.5.cloned.1.call-done, f32[256]{0:T(256)S(1)} %dynamic-slice_convert_fusion.1), kind=kOutput, calls=%fused_computation.38 | convolution fusion | flops 1342308352 | bytes 8389632 | tf_op jit(solution)/shard_map/dot_general | solution.py:89
  117.4 1.0 fusion.28
  118.7 8.4 %all_gather.20 = bf16[2048,128]{0,1:T(8,128)(2,1)S(1)} all-gather(bf16[512,128]{0,1:T(8,128)(2,1)S(1)} %get-tuple-element.284), channel_id=1, replica_groups=mesh['blk'=4,'tp'=8] {'blk'}, dimensions={0}, use_global_device_ids=true | all-gather | bytes 655360 | tf_op jit(solution)/shard_map/all_gather | solution.py:118
  127.1 12.1 %all_gather.22 = bf16[2048,128]{0,1:T(8,128)(2,1)} all-gather(bf16[512,128]{0,1:T(8,128)(2,1)S(1)} %slice.41), channel_id=1, replica_groups=mesh['blk'=4,'tp'=8] {'blk'}, dimensions={0}, use_global_device_ids=true | all-gather | bytes 655360 | tf_op jit(solution)/shard_map/all_gather | solution.py:119
  139.3 7.9 %convolution_add_fusion = f32[512,512]{0,1:T(8,128)} fusion(bf16[512,5120]{0,1:T(8,128)(2,1)} %bitcast_select_fusion.1, bf16[5120,512]{1,0:T(8,128)(2,1)} %all-gather.7.cloned.1.call-done, f32[512]{0:T(512)S(1)} %dynamic-slice_convert_fusion), kind=kOutput, calls=%fused_computation.37 | convolution fusion | flops 2684616704 | bytes 11536384 | tf_op jit(solution)/shard_map/dot_general | solution.py:84
  147.2 1.5 copy.45
  148.8 0.3 slice_negate_fusion
  149.1 0.4 fusion.26
  149.5 41.8 %while.18 = (s32[]{:T(128)}, f32[4,512]{1,0:T(4,128)S(1)}, f32[4,512]{1,0:T(4,128)S(1)}, f32[4,512,128]{2,1,0:T(8,128)}, s32[2048]{0:T(1024)S(1)}, /*index=5*/s3...) while((s32[]{:T(128)}, f32[4,512]{1,0:T(4,128)S(1)}, ...), condition=%wide.region_4.5_spmd.clone, body=%wide.region_1.4_spmd.clone.sunk | while | flops 552086528 | bytes 41828644 | solution.py:151
  149.9 2.9 fusion.49
  152.9 3.4 %fusion.50 = f32[4,512]{1,0:T(4,128)S(1)} fusion(f32[512,512,4]{1,0,2:T(8,128)} %get-tuple-element.356, f32[4,512]{1,0:T(4,128)S(1)} %select_maximum_fusion.2, pred[512,512]{0,1:T(8,128)(4,1)S(1)} %compare_and_fusion.3), kind=kLoop, calls=%fused_computation.6.clone.1 | loop fusion | flops 5240832 | bytes 4472832 | tf_op jit(solution)/shard_map/while/body/eval_jaxpr/reduce_sum | solution.py:142
  156.4 2.6 fusion.52
  159.0 1.0 copy-done.6
  160.4 3.0 fusion.49
  163.4 3.4 %fusion.50 = f32[4,512]{1,0:T(4,128)S(1)} fusion(f32[512,512,4]{1,0,2:T(8,128)} %get-tuple-element.356, f32[4,512]{1,0:T(4,128)S(1)} %select_maximum_fusion.2, pred[512,512]{0,1:T(8,128)(4,1)S(1)} %compare_and_fusion.3), kind=kLoop, calls=%fused_computation.6.clone.1 | loop fusion | flops 5240832 | bytes 4472832 | tf_op jit(solution)/shard_map/while/body/eval_jaxpr/reduce_sum | solution.py:142
  166.8 2.6 fusion.52
  169.5 1.0 copy-done.6
  170.8 2.9 fusion.49
  173.8 3.4 %fusion.50 = f32[4,512]{1,0:T(4,128)S(1)} fusion(f32[512,512,4]{1,0,2:T(8,128)} %get-tuple-element.356, f32[4,512]{1,0:T(4,128)S(1)} %select_maximum_fusion.2, pred[512,512]{0,1:T(8,128)(4,1)S(1)} %compare_and_fusion.3), kind=kLoop, calls=%fused_computation.6.clone.1 | loop fusion | flops 5240832 | bytes 4472832 | tf_op jit(solution)/shard_map/while/body/eval_jaxpr/reduce_sum | solution.py:142
  177.2 2.6 fusion.52
  179.9 1.0 copy-done.6
  181.2 3.0 fusion.49
  184.2 3.4 %fusion.50 = f32[4,512]{1,0:T(4,128)S(1)} fusion(f32[512,512,4]{1,0,2:T(8,128)} %get-tuple-element.356, f32[4,512]{1,0:T(4,128)S(1)} %select_maximum_fusion.2, pred[512,512]{0,1:T(8,128)(4,1)S(1)} %compare_and_fusion.3), kind=kLoop, calls=%fused_computation.6.clone.1 | loop fusion | flops 5240832 | bytes 4472832 | tf_op jit(solution)/shard_map/while/body/eval_jaxpr/reduce_sum | solution.py:142
  187.7 2.6 fusion.52
  190.3 1.0 copy-done.6
  191.3 1.6 copy.51
  193.0 7.3 %convolution_convert_fusion = bf16[512,5120]{1,0:T(8,128)(2,1)} fusion(bf16[512,512]{0,1:T(8,128)(2,1)S(1)} %bitcast.102, bf16[512,5120]{0,1:T(8,128)(2,1)} %all-gather.9.cloned.1.call-done), kind=kOutput, calls=%fused_computation.33 | convolution fusion | flops 2686976000 | bytes 11010048 | tf_op jit(solution)/shard_map/dot_general | solution.py:160
  200.3 7.9 %copy.54 = bf16[512,5120]{0,1:T(8,128)(2,1)} copy(bf16[512,5120]{1,0:T(8,128)(2,1)} %convolution_convert_fusion) | data formatting | bytes 10485760
  208.3 104.8 %reduce-scatter.4.cloned.1.call-done = bf16[640,512]{1,0:T(8,128)(2,1)} async-done(((bf16[5120,512]{1,0:T(8,128)(2,1)}), bf16[640,512]{1,0:T(8,128)(2,1)}) %reduce-scatter.4.cloned.1.call-update) | async-done | bytes 655376
  313.1 1.4 copy.55
  314.5 2.1 add_convert_fusion
  (95 shorter events, 2.9 us)
Async XLA Ops:
  6.5 29.1 %copy-start.3 = (bf16[160,4096]{1,0:T(8,128)(2,1)S(1)}, bf16[160,4096]{1,0:T(8,128)(2,1)}, u32[]{:S(2)}) copy-start(bf16[160,4096]{1,0:T(8,128)(2,1)} %param.14) | copy-start | bytes 3932164
  6.5 105.9 %all-gather.5.cloned.1.call-start = ((), (), s32[]{:S(2)}) async-start(), calls=%async_computation.4 | async-start | bytes 3276800 | tf_op jit(solution)/shard_map/all_gather | solution.py:91
  7.8 62.4 %copy-start.4 = (bf16[4096,160]{0,1:T(8,128)(2,1)S(1)}, bf16[4096,160]{0,1:T(8,128)(2,1)}, u32[]{:S(2)}) copy-start(bf16[4096,160]{0,1:T(8,128)(2,1)} %param.18) | copy-start | bytes 3932164
  32.8 106.4 %all-gather.7.cloned.1.call-start = ((), (), s32[]{:S(2)}) async-start(), calls=%async_computation.5 | async-start | bytes 6553600 | tf_op jit(solution)/shard_map/all_gather | solution.py:86
  71.5 39.8 %all-to-all-start.2 = ((bf16[8,512,160]{1,2,0:T(8,128)(2,1)}), bf16[8,512,160]{1,2,0:T(8,128)(2,1)S(1)}, u32[]{:S(2)}, u32[]{:S(2)}) async-start(bf16[8,512,160]{1,2,0:T(8,128)(2,1)} %bitcast.78), calls=%async_computation.2 | async-start | bytes 2621440 | tf_op jit(solution)/shard_map/all_to_all | solution.py:159
  75.1 8.2 %copy-start.8 = (bf16[5120]{0:T(1024)(128)(2,1)S(1)}, bf16[5120]{0:T(1024)(128)(2,1)}, u32[]{:S(2)}) copy-start(bf16[5120]{0:T(1024)(128)(2,1)} %param.13) | copy-start | bytes 30724
  75.1 117.9 %all-gather.9.cloned.1.call-start = ((), (), s32[]{:S(2)}) async-start(), calls=%async_computation.6 | async-start | bytes 6553600 | tf_op jit(solution)/shard_map/all_gather | solution.py:162
  83.3 4.1 %copy-start.1 = (bf16[512,5120]{0,1:T(8,128)(2,1)S(1)}, bf16[512,5120]{0,1:T(8,128)(2,1)}, u32[]{:S(2)}) copy-start(bf16[512,5120]{0,1:T(8,128)(2,1)} %copy.42) | copy-start | bytes 15728644
  87.3 3.9 %copy-start.10 = (s32[32]{0:T(128)S(1)}, s32[32]{0:T(128)}, u32[]{:S(2)}) copy-start(s32[32]{0:T(128)} %param.19) | copy-start | bytes 388
  87.4 4.2 %copy-start.9 = (s32[512]{0:T(512)S(1)}, s32[512]{0:T(512)}, u32[]{:S(2)}) copy-start(s32[512]{0:T(512)} %param.20) | copy-start | bytes 6148
  91.6 5.6 %copy-start.7 = (s32[512]{0:T(512)S(1)}, s32[512]{0:T(512)}, u32[]{:S(2)}) copy-start(s32[512]{0:T(512)} %param.21) | copy-start | bytes 6148
  111.3 1.1 copy-start.2
  112.4 200.7 %reduce-scatter.4.cloned.1.call-start = ((), (), s32[]{:S(2)}) async-start(), calls=%async_computation.7 | async-start | bytes 5898240
  149.9 6.4 %copy-start.5 = (f32[4,512,128]{2,1,0:T(8,128)S(1)}, f32[4,512,128]{2,1,0:T(8,128)}, u32[]{:S(2)}) copy-start(f32[4,512,128]{2,1,0:T(8,128)} %get-tuple-element.376) | copy-start | bytes 3145732 | tf_op jit(solution)/shard_map/while
  152.9 3.5 %copy-start = (f32[512,512,4]{1,0,2:T(8,128)S(1)}, f32[512,512,4]{1,0,2:T(8,128)}, u32[]{:S(2)}) copy-start(f32[512,512,4]{1,0,2:T(8,128)} %get-tuple-element.356) | copy-start | bytes 12582916 | tf_op jit(solution)/shard_map/while
  159.0 1.0 copy-start.6
  160.4 6.4 %copy-start.5 = (f32[4,512,128]{2,1,0:T(8,128)S(1)}, f32[4,512,128]{2,1,0:T(8,128)}, u32[]{:S(2)}) copy-start(f32[4,512,128]{2,1,0:T(8,128)} %get-tuple-element.376) | copy-start | bytes 3145732 | tf_op jit(solution)/shard_map/while
  163.4 3.4 %copy-start = (f32[512,512,4]{1,0,2:T(8,128)S(1)}, f32[512,512,4]{1,0,2:T(8,128)}, u32[]{:S(2)}) copy-start(f32[512,512,4]{1,0,2:T(8,128)} %get-tuple-element.356) | copy-start | bytes 12582916 | tf_op jit(solution)/shard_map/while
  169.5 1.0 copy-start.6
  170.8 6.4 %copy-start.5 = (f32[4,512,128]{2,1,0:T(8,128)S(1)}, f32[4,512,128]{2,1,0:T(8,128)}, u32[]{:S(2)}) copy-start(f32[4,512,128]{2,1,0:T(8,128)} %get-tuple-element.376) | copy-start | bytes 3145732 | tf_op jit(solution)/shard_map/while
  173.8 3.4 %copy-start = (f32[512,512,4]{1,0,2:T(8,128)S(1)}, f32[512,512,4]{1,0,2:T(8,128)}, u32[]{:S(2)}) copy-start(f32[512,512,4]{1,0,2:T(8,128)} %get-tuple-element.356) | copy-start | bytes 12582916 | tf_op jit(solution)/shard_map/while
  179.9 1.0 copy-start.6
  181.2 6.4 %copy-start.5 = (f32[4,512,128]{2,1,0:T(8,128)S(1)}, f32[4,512,128]{2,1,0:T(8,128)}, u32[]{:S(2)}) copy-start(f32[4,512,128]{2,1,0:T(8,128)} %get-tuple-element.376) | copy-start | bytes 3145732 | tf_op jit(solution)/shard_map/while
  184.2 3.4 %copy-start = (f32[512,512,4]{1,0,2:T(8,128)S(1)}, f32[512,512,4]{1,0,2:T(8,128)}, u32[]{:S(2)}) copy-start(f32[512,512,4]{1,0,2:T(8,128)} %get-tuple-element.356) | copy-start | bytes 12582916 | tf_op jit(solution)/shard_map/while
  190.3 1.0 copy-start.6
Sparse Core Ops, SparseCore 0:
  32.9 24.1 all-gather.4
  70.3 39.4 all-gather.6
  112.5 45.1 all-gather.8
  208.4 104.6 reduce-scatter.3
